TPU v7x, 32 devices: a whole 2x2x4 slice. The times are simulated.
32 devices in a mesh: groups: 2 (over x), row: 16 (over z, y, core).
Axes of the slice: x: 2, y: 2, z: 4, core: 2. Of those that a mesh axis runs over, the one named last changes fastest.
Arguments:
- latent: bfloat16 [8, 16, 128, 16], P('groups', None, 'row'), parts along dimension 0, may hold values from -16 to 16, as said below
- w_in: bfloat16 [3, 3, 3, 16, 384], replicated, may hold values from -0.3125 to 0.3125
- gain_one: float32 [384], replicated, may hold values from 0.25 to 1.75
- w_mid: bfloat16 [3, 3, 3, 384, 384], replicated, may hold values from -0.0625 to 0.0625
- gain_two: float32 [384], replicated, may hold values from 0.25 to 1.75
- w_up: bfloat16 [3, 3, 384, 192], replicated, may hold values from -0.109375 to 0.109375
- gain_three: float32 [192], replicated, may hold values from 0.25 to 1.75
- w_low: bfloat16 [3, 3, 3, 192, 96], replicated, may hold values from -0.078125 to 0.078125
- gain_four: float32 [96], replicated, may hold values from 0.25 to 1.75
- w_out: bfloat16 [3, 3, 3, 96, 3], replicated, may hold values from -0.125 to 0.125
Outputs:
- frames_rgb: float32 [8, 3, 32, 256], P('groups', None, 'row'), parts along dimension 0
There are 2 independent parts, one for each index of `groups`. A program takes and returns all parts, laid end to end along the dimension named above; an argument that names none is the same for every part. Nothing has to cross between parts.
Inputs may be any that keep to these rules, and one draw needn't show every extreme that they name: latent is real-valued.
All inputs are finite; a program needn't handle non-finite values.
Results may differ from a plain program's by a relative error of at most 0.0058.
Values may be sent and summed in bfloat16 or wider, within the bound.
A program may use at most 128 MiB of HBM per device.

v0:
```python
import functools

import jax
import jax.numpy as jnp
from jax import lax
from jax.experimental import pallas as pl
from jax.experimental.pallas import tpu as pltpu
from jax.sharding import PartitionSpec as P

eps = 1e-06
f32, bf16 = jnp.float32, jnp.bfloat16


def silu(z):
    return z / (1.0 + jnp.exp(-z))


def rms_act(field, gain):
    mean = jnp.mean(field * field, axis=-1, keepdims=True)
    return silu(field * lax.rsqrt(mean + eps) * gain)


def pair_norm(field, gain, low):
    half = field.shape[-1] // 2
    square = field * field
    first = jnp.sum(jnp.where(low, square, 0.0), axis=-1, keepdims=True)
    second = jnp.sum(jnp.where(low, 0.0, square), axis=-1, keepdims=True)
    scale = jnp.where(low, lax.rsqrt(first / half + eps), lax.rsqrt(second / half + eps))
    return silu(field * scale * gain)


def dot(a, b):
    return jnp.dot(a, b, preferred_element_type=f32)


def kernel(
    sizes, devices,
    g_ref, g1_ref, g2_ref, g3_ref, g4_ref,
    win_hbm, wmid_hbm, wup_hbm, wlow_hbm, wout_ref,
    out_ref,
    win, wmid, wup, wlow,
    gs, a1, first_mid, b0, b1, sent, a3, a3s, ys, part, got,
    wsem, send_sem, recv_sem, psend, precv,
):
    frames, cols, c1, c2, c3, tall = sizes
    me = lax.axis_index("row")
    is_first, is_last = me == 0, me == devices - 1
    has_up, has_down = me > 0, me < devices - 1

    copies = [pltpu.make_async_copy(win_hbm, win, wsem.at[0])]
    for i, a in enumerate((2, 1, 0)):
        copies.append(pltpu.make_async_copy(wmid_hbm.at[a], wmid.at[a], wsem.at[1 + i]))
    copies.append(pltpu.make_async_copy(wup_hbm, wup, wsem.at[4]))
    copies.append(pltpu.make_async_copy(wlow_hbm, wlow, wsem.at[5]))
    for copy in copies:
        copy.start()

    barrier = pltpu.get_barrier_semaphore()

    @pl.when(has_up)
    def _():
        pl.semaphore_signal(barrier, inc=1, device_id={"row": me - 1}, device_id_type=pl.DeviceIdType.MESH)

    @pl.when(has_down)
    def _():
        pl.semaphore_signal(barrier, inc=1, device_id={"row": me + 1}, device_id_type=pl.DeviceIdType.MESH)

    pl.semaphore_wait(barrier, has_up.astype(jnp.int32) + has_down.astype(jnp.int32))

    for t in range(frames):
        b1[t, cols:tall, :] = jnp.zeros((tall - cols, 3 * c1), bf16)

    @pl.when(is_first)
    def _():
        for t in range(frames):
            b1[t, 0:cols, 0:c1] = jnp.zeros((cols, c1), bf16)
        got[0] = jnp.zeros(got.shape[1:], f32)

    @pl.when(is_last)
    def _():
        for t in range(frames):
            b1[t, 0:cols, 2 * c1 : 3 * c1] = jnp.zeros((cols, c1), bf16)
        got[1] = jnp.zeros(got.shape[1:], f32)

    row_id = lax.broadcasted_iota(jnp.int32, (cols, 1), 0)
    lanes = g_ref.shape[-1]
    for t in range(frames):
        g = g_ref[t].astype(f32)
        left = jnp.where(row_id == 0, 0.0, pltpu.roll(g, 1, 0))
        right = jnp.where(row_id == cols - 1, 0.0, pltpu.roll(g, cols - 1, 0))
        gs[t, :, 0:lanes] = left.astype(bf16)
        gs[t, :, lanes : 2 * lanes] = g.astype(bf16)
        gs[t, :, 2 * lanes : 3 * lanes] = right.astype(bf16)

    copies[0].wait()
    for b in range(3):
        keep = None if b == 1 else (has_up if b == 0 else has_down).astype(f32)
        for t in range(frames):
            total = None
            for a in range(3):
                s = t + a - 2
                if s >= 0:
                    d = dot(gs[s], win[a, :, b * c1 : (b + 1) * c1])
                    total = d if total is None else total + d
            if b == 1:
                first_mid[t] = total
            act = rms_act(total, g1_ref[...])
            if keep is not None:
                act = act * keep
            left = jnp.where(row_id == 0, 0.0, pltpu.roll(act, 1, 0))
            right = jnp.where(row_id == cols - 1, 0.0, pltpu.roll(act, cols - 1, 0))
            base = 3 * b * c1
            a1[t, :, base : base + c1] = left.astype(bf16)
            a1[t, :, base + c1 : base + 2 * c1] = act.astype(bf16)
            a1[t, :, base + 2 * c1 : base + 3 * c1] = right.astype(bf16)

    def halo(t, down):
        lane = 0 if down else 2 * c1
        peer = me + 1 if down else me - 1
        return pltpu.make_async_remote_copy(
            src_ref=sent.at[t],
            dst_ref=b1.at[t, pl.ds(0, cols), pl.ds(lane, c1)],
            send_sem=send_sem.at[int(down), t],
            recv_sem=recv_sem.at[int(down), t],
            device_id={"row": peer},
            device_id_type=pl.DeviceIdType.MESH,
        )

    waited = set()
    for t in range(frames):
        total = first_mid[t]
        for i, a in enumerate((2, 1, 0)):
            s = t + a - 2
            if s >= 0:
                if a not in waited:
                    waited.add(a)
                    copies[1 + i].wait()
                total = total + dot(a1[s], wmid[a])
        act = rms_act(total, g2_ref[...]).astype(bf16)
        sent[t] = act
        b1[t, 0:cols, c1 : 2 * c1] = act

        @pl.when(has_down)
        def _(t=t):
            halo(t, True).start()

        @pl.when(has_up)
        def _(t=t):
            halo(t, False).start()

    for i, a in enumerate((2, 1, 0)):
        if a not in waited:
            copies[1 + i].wait()
    copies[4].wait()
    copies[5].wait()

    lane3 = lax.broadcasted_iota(jnp.int32, (1, 2 * c2), 1)
    low3 = lane3 < c2
    tall_id = lax.broadcasted_iota(jnp.int32, (tall, 1), 0)
    keep_up, keep_down = has_up.astype(f32), has_down.astype(f32)
    lane4 = lax.broadcasted_iota(jnp.int32, (1, cols), 1)
    block = ys.shape[2] // 9

    def send_part(t, down):
        peer = me + 1 if down else me - 1
        return pltpu.make_async_remote_copy(
            src_ref=part.at[0 if down else 1, t],
            dst_ref=got.at[0 if down else 1, t],
            send_sem=psend.at[int(down), t],
            recv_sem=precv.at[int(down), t],
            device_id={"row": peer},
            device_id_type=pl.DeviceIdType.MESH,
        )

    for t in range(frames):
        @pl.when(has_up)
        def _(t=t):
            halo(t, True).wait_recv()

        @pl.when(has_down)
        def _(t=t):
            halo(t, False).wait_recv()

        b0[t] = pltpu.roll(b1[t].astype(f32), 1, 0).astype(bf16)
        for p in range(2):
            span = slice(p * c1, p * c1 + 2 * c1)
            third = dot(b0[t, :, span], wup[0]) + dot(b1[t, :, span], wup[1])
            for parity in range(2):
                field = third[:, parity * 2 * c2 : (parity + 1) * 2 * c2]
                act = pair_norm(field, g3_ref[...], low3)
                edge = keep_up if p == 0 else keep_down
                outer = low3 if p == 0 else jnp.logical_not(low3)
                act = act * jnp.where(outer, edge, 1.0)
                drop = 0 if parity == 0 else cols
                act = jnp.where(tall_id == drop, 0.0, act)
                base = parity * 4 * c2 + p * 2 * c2
                a3[t, :, base : base + 2 * c2] = act.astype(bf16)
                a3s[t, :, base : base + 2 * c2] = pltpu.roll(act, tall - 1, 0).astype(bf16)

        for parity in range(2):
            total = None
            for a in range(3):
                s = t + a - 2
                if s < 0:
                    continue
                if parity == 0:
                    d = dot(a3[s, 0:cols, :], wlow[a, 0 : 8 * c2, :])
                    d += dot(a3s[s, 0:cols, 0 : 4 * c2], wlow[a, 8 * c2 : 12 * c2, :])
                else:
                    d = dot(a3[s, 0:cols, 4 * c2 : 8 * c2], wlow[a, 0 : 4 * c2, :])
                    d += dot(a3s[s, 0:cols, :], wlow[a, 4 * c2 : 12 * c2, :])
                total = d if total is None else total + d
            acts = []
            half = total.shape[-1] // 2
            for q in range(2):
                field = total[:, q * half : (q + 1) * half]
                mean = jnp.sum(field * field, axis=-1, keepdims=True) / c3
                acts.append(silu(field * lax.rsqrt(mean + eps) * g4_ref[...]).astype(bf16))
            act = jnp.concatenate(acts, axis=-1)
            ys[t, parity] = lax.dot_general(
                wout_ref[...], act, (((1,), (1,)), ((), ())), preferred_element_type=f32
            )

        even, odd = None, None
        for a in range(3):
            s = t + a - 2
            if s < 0:
                continue
            taps = [[ys[s, parity, (3 * a + e) * block : (3 * a + e + 1) * block, :] for e in range(3)] for parity in range(2)]
            before = jnp.where(lane4 == 0, 0.0, pltpu.roll(taps[1][0], 1, 1))
            after = jnp.where(lane4 == cols - 1, 0.0, pltpu.roll(taps[0][2], cols - 1, 1))
            new_even = before + taps[0][1] + taps[1][2]
            new_odd = taps[0][0] + taps[1][1] + after
            even = new_even if even is None else even + new_even
            odd = new_odd if odd is None else odd + new_odd
        rows = block // 4
        for parity, value in enumerate((even, odd)):
            part[1, t, parity] = value[0:rows]
            part[0, t, parity] = value[3 * rows : 4 * rows]
            out_ref[t, parity] = value[rows : 3 * rows]

        @pl.when(has_down)
        def _(t=t):
            send_part(t, True).start()

        @pl.when(has_up)
        def _(t=t):
            send_part(t, False).start()

    for t in range(frames):
        @pl.when(has_up)
        def _(t=t):
            send_part(t, True).wait_recv()
            halo(t, False).wait_send()
            send_part(t, False).wait_send()

        @pl.when(has_down)
        def _(t=t):
            send_part(t, False).wait_recv()
            halo(t, True).wait_send()
            send_part(t, True).wait_send()

        rows = block // 4
        for parity in range(2):
            out_ref[t, parity, 0:rows] += got[0, t, parity]
            out_ref[t, parity, rows : 2 * rows] += got[1, t, parity]


def per_device(latent, w_in, gain_one, w_mid, gain_two, w_up, gain_three, w_low, gain_four, w_out):
    frames, height, tw, c0 = latent.shape
    devices = lax.axis_size("row")
    cols = tw * devices
    assert height == devices
    c1, c2, c3 = w_in.shape[-1], w_up.shape[-1], w_low.shape[-1]
    colours = w_out.shape[-1]
    tall = cols + 16
    half, rows = 128, 8

    padded = jnp.pad(latent, ((0, 0), (2, 2), (0, 0), (0, 0)))
    stacked = jnp.stack([padded[:, s : s + height] for s in range(5)], axis=3)
    blocks = jnp.transpose(stacked, (1, 0, 2, 3, 4)).reshape(height, frames, tw, 5 * c0)
    arrived = lax.all_to_all(blocks, "row", split_axis=0, concat_axis=0, tiled=True)
    g = jnp.transpose(arrived, (1, 0, 2, 3)).reshape(frames, cols, 5 * c0)
    lanes = -(-5 * c0 // 128) * 128
    g = jnp.pad(g, ((0, 0), (0, 0), (0, lanes - 5 * c0)))

    tap = jnp.transpose(w_in, (0, 2, 1, 3, 4)).reshape(3, 3, 3 * c0, c1)
    win = jnp.concatenate(
        [jnp.pad(tap, ((0, 0), (0, 0), (b * c0, lanes - (3 + b) * c0), (0, 0))) for b in range(3)], axis=-1
    ).reshape(3, 3 * lanes, 3 * c1)
    wmid = w_mid.reshape(3, 9 * c1, c1)

    wide = w_up.astype(f32)

    def fold(w, axis):
        k0, k1, k2 = (lax.index_in_dim(w, i, axis, keepdims=False) for i in range(3))
        return ((k0 + k1, k0), (k2, k1 + k2))

    folded = []
    by_row = fold(wide, 0)
    for in_col in range(2):
        in_rows = []
        for in_row in range(2):
            outs = [fold(by_row[in_row][out_row], 0)[in_col][parity] for parity in range(2) for out_row in range(2)]
            in_rows.append(jnp.concatenate(outs, axis=-1))
        folded.append(jnp.concatenate(in_rows, axis=0))
    wup = jnp.stack(folded).astype(bf16)

    tap = jnp.transpose(w_low, (0, 2, 1, 3, 4)).reshape(3, 3, 3 * c2, c3)
    tap = jnp.pad(tap, ((0, 0), (0, 0), (0, 0), (0, half - c3)))
    wlow = jnp.concatenate(
        [jnp.pad(tap, ((0, 0), (0, 0), (q * c2, (1 - q) * c2), (0, 0))) for q in range(2)], axis=-1
    ).reshape(3, 12 * c2, 2 * half)

    tap = jnp.transpose(w_out, (0, 2, 1, 4, 3))
    tap = jnp.pad(tap, ((0, 0), (0, 0), (0, 0), (0, rows - colours), (0, half - c3)))
    zero = jnp.zeros((3, 3, rows, half), bf16)
    by_slot = []
    for slot in range(4):
        sides = []
        for q in range(2):
            b = q - slot + 2
            sides.append(tap[:, :, b] if 0 <= b <= 2 else zero)
        by_slot.append(jnp.concatenate(sides, axis=-1))
    wout = jnp.stack(by_slot, axis=2).reshape(9 * 4 * rows, 2 * half)

    gain_pair = jnp.concatenate([gain_three, gain_three]).reshape(1, 2 * c2)
    gain_last = jnp.pad(gain_four, (0, half - c3)).reshape(1, half)

    vmem = pl.BlockSpec(memory_space=pltpu.VMEM)
    any_space = pl.BlockSpec(memory_space=pl.ANY)
    out = pl.pallas_call(
        functools.partial(kernel, (frames, cols, c1, c2, c3, tall), devices),
        out_shape=jax.ShapeDtypeStruct((frames, 2, 2 * rows, cols), f32),
        in_specs=[vmem] * 5 + [any_space] * 4 + [vmem],
        out_specs=vmem,
        scratch_shapes=[
            pltpu.VMEM(win.shape, bf16),
            pltpu.VMEM(wmid.shape, bf16),
            pltpu.VMEM(wup.shape, bf16),
            pltpu.VMEM(wlow.shape, bf16),
            pltpu.VMEM((frames, cols, 3 * lanes), bf16),
            pltpu.VMEM((frames, cols, 9 * c1), bf16),
            pltpu.VMEM((frames, cols, c1), f32),
            pltpu.VMEM((frames, tall, 3 * c1), bf16),
            pltpu.VMEM((frames, tall, 3 * c1), bf16),
            pltpu.VMEM((frames, cols, c1), bf16),
            pltpu.VMEM((frames, tall, 8 * c2), bf16),
            pltpu.VMEM((frames, tall, 8 * c2), bf16),
            pltpu.VMEM((frames, 2, 9 * 4 * rows, cols), f32),
            pltpu.VMEM((2, frames, 2, rows, cols), f32),
            pltpu.VMEM((2, frames, 2, rows, cols), f32),
            pltpu.SemaphoreType.DMA((6,)),
            pltpu.SemaphoreType.DMA((2, frames)),
            pltpu.SemaphoreType.DMA((2, frames)),
            pltpu.SemaphoreType.DMA((2, frames)),
            pltpu.SemaphoreType.DMA((2, frames)),
        ],
        compiler_params=pltpu.CompilerParams(
            collective_id=0, has_side_effects=True, vmem_limit_bytes=60 * 1024 * 1024
        ),
    )(
        g, gain_one.reshape(1, c1), gain_two.reshape(1, c1), gain_pair, gain_last,
        win, wmid, wup, wlow, wout,
    )
    out = out.reshape(frames, 2, 2, rows, cols)[:, :, :, :colours]
    return jnp.transpose(out, (0, 3, 2, 4, 1)).reshape(frames, colours, 2, 2 * cols)


def solution(mesh):
    placed = (P("groups", None, "row", None), P(), P(), P(), P(), P(), P(), P(), P(), P())
    return jax.shard_map(
        per_device,
        mesh=mesh,
        in_specs=placed,
        out_specs=P("groups", None, "row", None),
        check_vma=False,
    )
```

profile of v0, /device:TPU:1, one launch (start us, length us, event | category | flops | bytes accessed | tf_op | source)
XLA Modules:
  0.0 57.9 jit_solution(6211254730475177798)
XLA Ops:
  0.0 1.0 %fusion.26 = bf16[4,16,8,5,16]{4,2,1,0,3:T(8,128)(2,1)S(1)} fusion(bf16[4,16,8,16]{3,2,1,0:T(8,128)(2,1)} %param.10), kind=kLoop, calls=%fused_computation.58 | loop fusion | bytes 147456
  1.0 0.9 %fusion.28 = bf16[4,16,8,5,16]{4,2,1,0,3:T(8,128)(2,1)S(1)} fusion(bf16[4,16,8,5,16]{4,2,1,0,3:T(8,128)(2,1)S(1)} %fusion.26, bf16[4,16,8,16]{3,2,1,0:T(8,128)(2,1)} %param.10), kind=kLoop, calls=%fused_computation.60 | loop fusion | bytes 147456
  2.0 0.9 %bitcast_dynamic-update-slice_fusion = bf16[4,16,8,5,16]{4,2,1,0,3:T(8,128)(2,1)S(1)} fusion(bf16[4,16,8,5,16]{4,2,1,0,3:T(8,128)(2,1)S(1)} %fusion.28, bf16[4,16,8,16]{3,2,1,0:T(8,128)(2,1)} %param.10), kind=kLoop, calls=%fused_computation.65 | loop fusion | bytes 147456
  2.9 0.9 %fusion.30 = bf16[4,16,8,5,16]{4,2,1,0,3:T(8,128)(2,1)S(1)} fusion(bf16[4,16,8,5,16]{4,2,1,0,3:T(8,128)(2,1)S(1)} %bitcast_dynamic-update-slice_fusion, bf16[4,16,8,16]{3,2,1,0:T(8,128)(2,1)} %param.10), kind=kLoop, calls=%fused_computation.62 | loop fusion | bytes 147456
  3.9 0.9 %fusion.32 = bf16[4,16,8,5,16]{4,2,1,0,3:T(8,128)(2,1)S(1)} fusion(bf16[4,16,8,5,16]{4,2,1,0,3:T(8,128)(2,1)S(1)} %fusion.30, bf16[4,16,8,16]{3,2,1,0:T(8,128)(2,1)} %param.10), kind=kLoop, calls=%fused_computation.64 | loop fusion | bytes 147456 | tf_op jit(solution)/shard_map/stack | solution.py:280
  4.8 0.8 %copy.16 = bf16[16,4,8,5,16]{4,3,2,1,0:T(8,128)(2,1)S(1)} copy(bf16[16,4,8,5,16]{4,2,0,1,3:T(8,128)(2,1)S(1)} %bitcast.101) | data formatting | bytes 163840 | tf_op jit(solution)/shard_map/transpose | solution.py:281
  5.6 1.2 %reshape.68 = bf16[16,4,8,80]{3,2,1,0:T(8,128)(2,1)} reshape(bf16[16,4,8,5,16]{4,3,2,1,0:T(8,128)(2,1)S(1)} %copy.16) | data formatting | bytes 163840 | tf_op jit(solution)/shard_map/reshape | solution.py:281
  6.8 7.3 %all-to-all-start = ((bf16[16,4,8,80]{3,2,1,0:T(8,128)(2,1)}), bf16[16,4,8,80]{3,2,1,0:T(8,128)(2,1)S(1)}, u32[]{:S(2)}, u32[]{:S(2)}) async-start(bf16[16,4,8,80]{3,2,1,0:T(8,128)(2,1)} %reshape.68), calls=%async_computation | async-start | bytes 262144 | tf_op jit(solution)/shard_map/all_to_all | solution.py:282
  14.1 0.9 %copy.19 = bf16[3,3,384,192]{3,2,1,0:T(8,128)(2,1)S(1)} copy(bf16[3,3,384,192]{2,3,1,0:T(8,128)(2,1)S(1)} %copy-done.1) | data formatting | bytes 2654208 | tf_op args[5]
  16.8 0.7 %copy.23 = bf16[3,3,4,8,256]{4,3,2,1,0:T(8,128)(2,1)} copy(bf16[3,3,4,8,256]{4,3,1,0,2:T(8,128)(2,1)S(1)} %pad_maximum_fusion.1) | data formatting | bytes 294912 | tf_op jit(solution)/shard_map/stack | solution.py:325
  17.9 2.3 %fusion.6 = bf16[3,3,768,256]{3,2,1,0:T(8,128)(2,1)} fusion(bf16[3,3,576,128]{3,2,1,0:T(8,128)(2,1)S(1)} %pad.48), kind=kLoop, calls=%fused_computation.12 | loop fusion | flops 14155776 | bytes 4866048 | tf_op jit(solution)/shard_map/concatenate | solution.py:311
  20.3 1.8 %fusion.8 = bf16[3,3,128,1152]{3,2,1,0:T(8,128)(2,1)} fusion(bf16[3,3,48,384]{3,2,1,0:T(8,128)(2,1)S(1)} %bitcast.99), kind=kLoop, calls=%fused_computation.14 | loop fusion | flops 18579456 | bytes 2985984 | tf_op jit(solution)/shard_map/concatenate | solution.py:288
  22.2 0.5 reshape.72.g3_ref
  22.7 0.6 reshape.70.g1_ref
  23.3 0.6 reshape.71.g2_ref
  23.9 0.6 %pad_bitcast_fusion.2.g4_ref = f32[1,128]{1,0:T(1,128)} fusion(f32[96]{0:T(128)S(1)} %copy-done.7), kind=kLoop, calls=%fused_computation.78 | loop fusion | bytes 896 | tf_op jit(solution)/shard_map/reshape | solution.py:328
  24.5 0.5 maximum_bitcast_fusion
  25.0 0.5 maximum_bitcast_fusion.1
  25.5 1.7 %pad_maximum_fusion.wup_hbm = bf16[2,768,768]{2,1,0:T(8,128)(2,1)} fusion(bf16[1,768,768]{2,1,0:T(8,128)(2,1)S(1)} %maximum_bitcast_fusion.1, bf16[1,768,768]{2,1,0:T(8,128)(2,1)S(1)} %maximum_bitcast_fusion), kind=kLoop, calls=%fused_computation.15 | loop fusion | flops 1179648 | bytes 4718592 | tf_op jit(solution)/shard_map/stack | solution.py:307
  27.2 0.7 %pad.43.g_ref = bf16[4,128,128]{2,1,0:T(8,128)(2,1)} pad(bf16[4,128,80]{2,1,0:T(8,128)(2,1)S(1)} %copy_bitcast_fusion, bf16[]{:T(256)} %constant.4.clone.1), padding=0_0x0_0x0_48 | pad | bytes 212994 | tf_op jit(solution)/shard_map/jit(_pad)/pad | solution.py:285
  27.9 27.8 %shard_map.100 = f32[4,2,16,128]{3,2,1,0:T(8,128)} custom-call(bf16[4,128,128]{2,1,0:T(8,128)(2,1)} %pad.43.g_ref, f32[1,384]{1,0:T(1,128)} %reshape.70.g1_ref, f32[1,384]{1,0:T(1,128)} %reshape.71.g2_ref, f32[1,384]{1,0:T(1,128)} %reshape.72.g3_ref, f32[1,128]{1,0:T(1,128)} %pad_bitcast_fusion.2.g4_ref, bf16[3,384,1152]{2,1,0:T(8,128)(2,1)} %bitcast.95, ...), custom_call_target="tpu_custom_call" | custom-call | tf_op jit(solution)/shard_map/pallas_call | solution.py:332
  55.7 0.8 %slice.141 = f32[4,2,2,3,128]{4,3,2,1,0:T(4,128)S(1)} slice(f32[4,2,2,8,128]{4,3,2,1,0:T(8,128)} %bitcast.103), slice={[0:4], [0:2], [0:2], [0:3], [0:128]} | slice | bytes 49152 | tf_op jit(solution)/shard_map/slice | solution.py:366
  56.6 0.5 copy.28
  57.1 0.9 %copy.25 = f32[4,3,2,256]{3,2,1,0:T(2,128)} copy(f32[4,3,2,256]{0,3,2,1:T(8,128)S(1)} %bitcast.98) | data formatting | bytes 49152 | tf_op jit(solution)/shard_map/reshape | solution.py:367
  (31 shorter events, 2.2 us)
Async XLA Ops:
  0.0 14.1 %copy-start.1 = (bf16[3,3,384,192]{2,3,1,0:T(8,128)(2,1)S(1)}, bf16[3,3,384,192]{2,3,1,0:T(8,128)(2,1)}, u32[]{:S(2)}) copy-start(bf16[3,3,384,192]{2,3,1,0:T(8,128)(2,1)} %param.15) | copy-start | bytes 3981316
  6.8 20.4 %all-to-all-start = ((bf16[16,4,8,80]{3,2,1,0:T(8,128)(2,1)}), bf16[16,4,8,80]{3,2,1,0:T(8,128)(2,1)S(1)}, u32[]{:S(2)}, u32[]{:S(2)}) async-start(bf16[16,4,8,80]{3,2,1,0:T(8,128)(2,1)} %reshape.68), calls=%async_computation | async-start | bytes 262144 | tf_op jit(solution)/shard_map/all_to_all | solution.py:282
  16.0 0.7 %copy-start.3 = (bf16[3,3,3,96,3]{3,4,2,1,0:T(4,128)(2,1)S(1)}, bf16[3,3,3,96,3]{3,4,2,1,0:T(4,128)(2,1)}, u32[]{:S(2)}) copy-start(bf16[3,3,3,96,3]{3,4,2,1,0:T(4,128)(2,1)} %param.19) | copy-start | bytes 46660
  16.1 1.4 %copy-start = (bf16[3,3,3,192,96]{4,3,2,1,0:T(8,128)(2,1)S(1)}, bf16[3,3,3,192,96]{4,3,2,1,0:T(8,128)(2,1)}, u32[]{:S(2)}) copy-start(bf16[3,3,3,192,96]{4,3,2,1,0:T(8,128)(2,1)} %param.17) | copy-start | bytes 2985988
  17.9 2.3 %copy-start.2 = (bf16[3,3,3,16,384]{4,3,2,1,0:T(8,128)(2,1)S(1)}, bf16[3,3,3,16,384]{4,3,2,1,0:T(8,128)(2,1)}, u32[]{:S(2)}) copy-start(bf16[3,3,3,16,384]{4,3,2,1,0:T(8,128)(2,1)} %param.11) | copy-start | bytes 995332
  20.2 1.9 %copy-start.6 = (f32[192]{0:T(256)S(1)}, f32[192]{0:T(256)}, u32[]{:S(2)}) copy-start(f32[192]{0:T(256)} %param.16) | copy-start | bytes 2308
  20.2 2.5 %copy-start.4 = (f32[384]{0:T(512)S(1)}, f32[384]{0:T(512)}, u32[]{:S(2)}) copy-start(f32[384]{0:T(512)} %param.12) | copy-start | bytes 4612
  20.2 3.1 %copy-start.5 = (f32[384]{0:T(512)S(1)}, f32[384]{0:T(512)}, u32[]{:S(2)}) copy-start(f32[384]{0:T(512)} %param.14) | copy-start | bytes 4612
  20.2 3.6 %copy-start.7 = (f32[96]{0:T(128)S(1)}, f32[96]{0:T(128)}, u32[]{:S(2)}) copy-start(f32[96]{0:T(128)} %param.18) | copy-start | bytes 1156
where the time goes:
time: 58.3 us; the launch traced here: 57.9 us
  Pallas kernels  27.8 us (48%)
  local copies, waits for them, and re-layouts  14.6 us (25%)
  other arithmetic  8 us (14%)
  starting transfers between devices  7.34 us (13%)
    pallas_call x1, Pallas kernels, per_device(): pl.pallas_call(functools.partial(kernel, (frames, cols, c1, c2, c3, tall)...  27.8 us
    all_to_all x1, starting transfers between devices, per_device(): lax.all_to_all(blocks, 'row', split_axis=0, concat_axis=0, tiled=True)  7.34 us
    unnamed x23, local copies, waits for them, and re-layouts  5.74 us
    another operation x3, other arithmetic, per_device(): wup = jnp.stack(folded).astype(bf16)  2.71 us
    concatenate x1, other arithmetic, per_device(): jnp.concatenate([jnp.pad(tap, ((0, 0), (0, 0), (q * c2, (1 - q) * c2), (0...  2.31 us
    concatenate x1, other arithmetic, per_device(): jnp.concatenate([jnp.pad(tap, ((0, 0), (0, 0), (b * c0, lanes - (3 + b) *...  1.81 us
  transfers between devices with their start and end apart: 1, of which 0 were waited for; matrix products, arithmetic and copies ran while one was open for 21% of the time, Pallas kernels for 0%

commit v1 on v0

--- a/solution.py
+++ b/solution.py
@@ -33,25 +33,32 @@
     return jnp.dot(a, b, preferred_element_type=f32)
 
 
+def dot_t(a, b):
+    return lax.dot_general(a, b, (((1,), (1,)), ((), ())), preferred_element_type=f32)
+
+
 def kernel(
     sizes, devices,
-    g_ref, g1_ref, g2_ref, g3_ref, g4_ref,
+    g_ref, gains_ref,
     win_hbm, wmid_hbm, wup_hbm, wlow_hbm, wout_ref,
     out_ref,
+    raw_in, raw_up, raw_low,
     win, wmid, wup, wlow,
     gs, a1, first_mid, b0, b1, sent, a3, a3s, ys, part, got,
     wsem, send_sem, recv_sem, psend, precv,
 ):
-    frames, cols, c1, c2, c3, tall = sizes
+    frames, cols, c0, c1, c2, c3, tall = sizes
+    g1, g2 = gains_ref[0:1, 0:c1], gains_ref[1:2, 0:c1]
+    g3, g4 = gains_ref[2:3, 0 : 2 * c2], gains_ref[3:4, 0 : wlow.shape[-1] // 2]
     me = lax.axis_index("row")
     is_first, is_last = me == 0, me == devices - 1
     has_up, has_down = me > 0, me < devices - 1
 
-    copies = [pltpu.make_async_copy(win_hbm, win, wsem.at[0])]
+    copies = [pltpu.make_async_copy(win_hbm, raw_in, wsem.at[0])]
+    copies.append(pltpu.make_async_copy(wup_hbm, raw_up, wsem.at[4]))
+    copies.append(pltpu.make_async_copy(wlow_hbm, raw_low, wsem.at[5]))
     for i, a in enumerate((2, 1, 0)):
         copies.append(pltpu.make_async_copy(wmid_hbm.at[a], wmid.at[a], wsem.at[1 + i]))
-    copies.append(pltpu.make_async_copy(wup_hbm, wup, wsem.at[4]))
-    copies.append(pltpu.make_async_copy(wlow_hbm, wlow, wsem.at[5]))
     for copy in copies:
         copy.start()
 
@@ -92,7 +99,49 @@
         gs[t, :, lanes : 2 * lanes] = g.astype(bf16)
         gs[t, :, 2 * lanes : 3 * lanes] = right.astype(bf16)
 
+    for a in range(3):
+        win[a] = jnp.zeros(win.shape[1:], bf16)
     copies[0].wait()
+    for a in range(3):
+        for e in range(3):
+            for b in range(3):
+                block = raw_in[a, b, e]
+                for slot in range(3):
+                    at = e * lanes + (slot + b) * c0
+                    win[a, at : at + c0, slot * c1 : (slot + 1) * c1] = block
+
+    copies[1].wait()
+    for slot in range(2):
+        for in_row in range(2):
+            mixed = []
+            for e in range(3):
+                if slot == 0:
+                    taps = (0, 1) if in_row == 0 else (2,)
+                else:
+                    taps = (0,) if in_row == 0 else (1, 2)
+                value = raw_up[taps[0], e].astype(f32)
+                for b in taps[1:]:
+                    value = value + raw_up[b, e].astype(f32)
+                mixed.append(value)
+            k0, k1, k2 = mixed
+            for parity in range(2):
+                pair = (k0 + k1, k2) if parity == 0 else (k0, k1 + k2)
+                at = parity * 2 * c2 + slot * c2
+                for in_col in range(2):
+                    wup[in_col, at : at + c2, in_row * c1 : (in_row + 1) * c1] = pair[in_col].astype(bf16)
+
+    for a in range(3):
+        wlow[a] = jnp.zeros(wlow.shape[1:], bf16)
+    copies[2].wait()
+    for a in range(3):
+        for e in range(3):
+            for b in range(3):
+                block = raw_low[a, b, e]
+                for q in range(2):
+                    at = (4 * e + q + b) * c2
+                    lane = q * (wlow.shape[-1] // 2)
+                    wlow[a, at : at + c2, lane : lane + c3] = block
+
     for b in range(3):
         keep = None if b == 1 else (has_up if b == 0 else has_down).astype(f32)
         for t in range(frames):
@@ -104,7 +153,7 @@
                     total = d if total is None else total + d
             if b == 1:
                 first_mid[t] = total
-            act = rms_act(total, g1_ref[...])
+            act = rms_act(total, g1)
             if keep is not None:
                 act = act * keep
             left = jnp.where(row_id == 0, 0.0, pltpu.roll(act, 1, 0))
@@ -134,9 +183,9 @@
             if s >= 0:
                 if a not in waited:
                     waited.add(a)
-                    copies[1 + i].wait()
+                    copies[3 + i].wait()
                 total = total + dot(a1[s], wmid[a])
-        act = rms_act(total, g2_ref[...]).astype(bf16)
+        act = rms_act(total, g2).astype(bf16)
         sent[t] = act
         b1[t, 0:cols, c1 : 2 * c1] = act
 
@@ -150,9 +199,7 @@
 
     for i, a in enumerate((2, 1, 0)):
         if a not in waited:
-            copies[1 + i].wait()
-    copies[4].wait()
-    copies[5].wait()
+            copies[3 + i].wait()
 
     lane3 = lax.broadcasted_iota(jnp.int32, (1, 2 * c2), 1)
     low3 = lane3 < c2
@@ -184,10 +231,10 @@
         b0[t] = pltpu.roll(b1[t].astype(f32), 1, 0).astype(bf16)
         for p in range(2):
             span = slice(p * c1, p * c1 + 2 * c1)
-            third = dot(b0[t, :, span], wup[0]) + dot(b1[t, :, span], wup[1])
+            third = dot_t(b0[t, :, span], wup[0]) + dot_t(b1[t, :, span], wup[1])
             for parity in range(2):
                 field = third[:, parity * 2 * c2 : (parity + 1) * 2 * c2]
-                act = pair_norm(field, g3_ref[...], low3)
+                act = pair_norm(field, g3, low3)
                 edge = keep_up if p == 0 else keep_down
                 outer = low3 if p == 0 else jnp.logical_not(low3)
                 act = act * jnp.where(outer, edge, 1.0)
@@ -215,7 +262,7 @@
             for q in range(2):
                 field = total[:, q * half : (q + 1) * half]
                 mean = jnp.sum(field * field, axis=-1, keepdims=True) / c3
-                acts.append(silu(field * lax.rsqrt(mean + eps) * g4_ref[...]).astype(bf16))
+                acts.append(silu(field * lax.rsqrt(mean + eps) * g4).astype(bf16))
             act = jnp.concatenate(acts, axis=-1)
             ys[t, parity] = lax.dot_general(
                 wout_ref[...], act, (((1,), (1,)), ((), ())), preferred_element_type=f32
@@ -276,41 +323,17 @@
     tall = cols + 16
     half, rows = 128, 8
 
-    padded = jnp.pad(latent, ((0, 0), (2, 2), (0, 0), (0, 0)))
-    stacked = jnp.stack([padded[:, s : s + height] for s in range(5)], axis=3)
-    blocks = jnp.transpose(stacked, (1, 0, 2, 3, 4)).reshape(height, frames, tw, 5 * c0)
+    flat = jnp.transpose(latent, (1, 0, 2, 3)).reshape(height, frames, tw * c0)
+    padded = jnp.pad(flat, ((2, 2), (0, 0), (0, 0)))
+    blocks = jnp.stack([padded[s : s + height] for s in range(5)], axis=1)
     arrived = lax.all_to_all(blocks, "row", split_axis=0, concat_axis=0, tiled=True)
-    g = jnp.transpose(arrived, (1, 0, 2, 3)).reshape(frames, cols, 5 * c0)
+    g = arrived.reshape(devices, 5, frames, tw, c0)
+    g = jnp.transpose(g, (2, 0, 3, 1, 4)).reshape(frames, cols, 5 * c0)
     lanes = -(-5 * c0 // 128) * 128
     g = jnp.pad(g, ((0, 0), (0, 0), (0, lanes - 5 * c0)))
 
-    tap = jnp.transpose(w_in, (0, 2, 1, 3, 4)).reshape(3, 3, 3 * c0, c1)
-    win = jnp.concatenate(
-        [jnp.pad(tap, ((0, 0), (0, 0), (b * c0, lanes - (3 + b) * c0), (0, 0))) for b in range(3)], axis=-1
-    ).reshape(3, 3 * lanes, 3 * c1)
     wmid = w_mid.reshape(3, 9 * c1, c1)
-
-    wide = w_up.astype(f32)
-
-    def fold(w, axis):
-        k0, k1, k2 = (lax.index_in_dim(w, i, axis, keepdims=False) for i in range(3))
-        return ((k0 + k1, k0), (k2, k1 + k2))
-
-    folded = []
-    by_row = fold(wide, 0)
-    for in_col in range(2):
-        in_rows = []
-        for in_row in range(2):
-            outs = [fold(by_row[in_row][out_row], 0)[in_col][parity] for parity in range(2) for out_row in range(2)]
-            in_rows.append(jnp.concatenate(outs, axis=-1))
-        folded.append(jnp.concatenate(in_rows, axis=0))
-    wup = jnp.stack(folded).astype(bf16)
-
-    tap = jnp.transpose(w_low, (0, 2, 1, 3, 4)).reshape(3, 3, 3 * c2, c3)
-    tap = jnp.pad(tap, ((0, 0), (0, 0), (0, 0), (0, half - c3)))
-    wlow = jnp.concatenate(
-        [jnp.pad(tap, ((0, 0), (0, 0), (q * c2, (1 - q) * c2), (0, 0))) for q in range(2)], axis=-1
-    ).reshape(3, 12 * c2, 2 * half)
+    wup = jnp.transpose(w_up, (0, 1, 3, 2))
 
     tap = jnp.transpose(w_out, (0, 2, 1, 4, 3))
     tap = jnp.pad(tap, ((0, 0), (0, 0), (0, 0), (0, rows - colours), (0, half - c3)))
@@ -324,21 +347,25 @@
         by_slot.append(jnp.concatenate(sides, axis=-1))
     wout = jnp.stack(by_slot, axis=2).reshape(9 * 4 * rows, 2 * half)
 
-    gain_pair = jnp.concatenate([gain_three, gain_three]).reshape(1, 2 * c2)
-    gain_last = jnp.pad(gain_four, (0, half - c3)).reshape(1, half)
+    longest = max(c1, 2 * c2)
+    gain_rows = (gain_one, gain_two, jnp.concatenate([gain_three, gain_three]), gain_four)
+    gains = jnp.stack([jnp.pad(v, (0, longest - v.shape[0])) for v in gain_rows])
 
     vmem = pl.BlockSpec(memory_space=pltpu.VMEM)
     any_space = pl.BlockSpec(memory_space=pl.ANY)
     out = pl.pallas_call(
-        functools.partial(kernel, (frames, cols, c1, c2, c3, tall), devices),
+        functools.partial(kernel, (frames, cols, c0, c1, c2, c3, tall), devices),
         out_shape=jax.ShapeDtypeStruct((frames, 2, 2 * rows, cols), f32),
-        in_specs=[vmem] * 5 + [any_space] * 4 + [vmem],
+        in_specs=[vmem] * 2 + [any_space] * 4 + [vmem],
         out_specs=vmem,
         scratch_shapes=[
-            pltpu.VMEM(win.shape, bf16),
+            pltpu.VMEM(w_in.shape, bf16),
+            pltpu.VMEM(wup.shape, bf16),
+            pltpu.VMEM(w_low.shape, bf16),
+            pltpu.VMEM((3, 3 * lanes, 3 * c1), bf16),
             pltpu.VMEM(wmid.shape, bf16),
-            pltpu.VMEM(wup.shape, bf16),
-            pltpu.VMEM(wlow.shape, bf16),
+            pltpu.VMEM((2, 4 * c2, 2 * c1), bf16),
+            pltpu.VMEM((3, 12 * c2, 2 * half), bf16),
             pltpu.VMEM((frames, cols, 3 * lanes), bf16),
             pltpu.VMEM((frames, cols, 9 * c1), bf16),
             pltpu.VMEM((frames, cols, c1), f32),
@@ -360,8 +387,7 @@
             collective_id=0, has_side_effects=True, vmem_limit_bytes=60 * 1024 * 1024
         ),
     )(
-        g, gain_one.reshape(1, c1), gain_two.reshape(1, c1), gain_pair, gain_last,
-        win, wmid, wup, wlow, wout,
+        g, gains, w_in, wmid, wup, w_low, wout,
     )
     out = out.reshape(frames, 2, 2, rows, cols)[:, :, :, :colours]
     return jnp.transpose(out, (0, 3, 2, 4, 1)).reshape(frames, colours, 2, 2 * cols)

time: 58.3 us -> 53.4 us (0.916)
  other arithmetic: 8 us -> 0.72 us
  local copies, waits for them, and re-layouts: 14.6 us -> 10.4 us
  waiting for transfers between devices: 0.01 us -> 3.97 us
  Pallas kernels: 27.8 us -> 30.5 us
    concatenate x3 -> x1, other arithmetic: 4.19 us -> 0.08 us  [per_device(): jnp.concatenate([gain_three, gain_three])]
    all_to_all x1, waiting for transfers between devices: 0.01 us -> 3.97 us  [per_device(): lax.all_to_all(blocks, 'row', split_axis=0, concat_axis=0, tiled=True)]
    unnamed x23 -> x13, local copies, waits for them, and re-layouts: 5.74 us -> 2.96 us
    pallas_call x1, Pallas kernels: 27.8 us -> 30.5 us  [per_device(): pl.pallas_call(functools.partial(kernel, (frames, cols, c0, c1, c2, c3, t...]
    another operation x5 -> x1, other arithmetic: 3.1 us -> 0.6 us  [per_device(): jnp.stack([jnp.pad(v, (0, longest - v.shape[0])) for v in gain_rows])]
    reshape x6 -> x3, local copies, waits for them, and re-layouts: 3.45 us -> 1.08 us  [the longest x1 0.51 us: per_device(): g = jnp.transpose(g, (2, 0, 3, 1, 4)).reshape(frames, cols, 5 * c0)]
    transpose x2, local copies, waits for them, and re-layouts: 0.9 us -> 1.79 us  [the longest x1 0.97 us: per_device(): flat = jnp.transpose(latent, (1, 0, 2, 3)).reshape(height, frames, tw * c0)]
    squeeze x1, local copies, waits for them, and re-layouts: 0.02 us -> 0.75 us  [per_device(): sides.append(tap[:, :, b] if 0 <= b <= 2 else zero)]
  transfers between devices with their start and end apart: 1 -> 1, of which waited for: 0 -> 1; matrix products, arithmetic and copies ran while one was open for 21% -> 4% of each run, Pallas kernels for 0% -> 0%
where the time goes in v1:
time: 53.4 us; the launch traced here: 53.1 us
  Pallas kernels  30.5 us (57%)
  local copies, waits for them, and re-layouts  10.4 us (19%)
  starting transfers between devices  7.34 us (14%)
  waiting for transfers between devices  3.97 us (7%)
  other arithmetic  0.72 us (1%)
    pallas_call x1, Pallas kernels, per_device(): pl.pallas_call(functools.partial(kernel, (frames, cols, c0, c1, c2, c3, t...  30.5 us
    all_to_all x1, starting transfers between devices, per_device(): lax.all_to_all(blocks, 'row', split_axis=0, concat_axis=0, tiled=True)  7.34 us
    all_to_all x1, waiting for transfers between devices, per_device(): lax.all_to_all(blocks, 'row', split_axis=0, concat_axis=0, tiled=True)  3.97 us
    unnamed x13, local copies, waits for them, and re-layouts  2.96 us
  transfers between devices with their start and end apart: 1, of which 1 were waited for; matrix products, arithmetic and copies ran while one was open for 4% of the time, Pallas kernels for 0%

profile of v1, /device:TPU:1, one launch (start us, length us, event | category | flops | bytes accessed | tf_op | source)
XLA Modules:
  0.0 53.1 jit_solution(8986383980854028317)
XLA Ops:
  0.0 0.0 copy-start.1
  0.0 1.0 %copy.21 = bf16[16,4,8,16]{3,2,1,0:T(8,128)(2,1)S(1)} copy(bf16[16,4,8,16]{3,2,0,1:T(8,128)(2,1)} %bitcast.56) | data formatting | bytes 32768 | tf_op jit(solution)/shard_map/transpose | solution.py:326
  1.0 0.1 reshape.22
  1.1 0.1 stack.50
  1.3 0.6 %bitcast_dynamic-update-slice_fusion.2 = bf16[16,5,4,128]{3,2,1,0:T(4,128)(2,1)} fusion(bf16[16,4,128]{2,1,0:T(4,128)(2,1)S(1)} %reshape.22), kind=kLoop, calls=%fused_computation.13 | loop fusion | bytes 32768
  1.9 0.6 %bitcast_dynamic-update-slice_fusion.1 = bf16[16,5,4,128]{3,2,1,0:T(4,128)(2,1)} fusion(bf16[16,5,4,128]{3,2,1,0:T(4,128)(2,1)} %bitcast_dynamic-update-slice_fusion.2, bf16[16,4,128]{2,1,0:T(4,128)(2,1)S(1)} %reshape.22), kind=kLoop, calls=%fused_computation.12 | loop fusion | bytes 32768
  2.5 0.6 %constant_dynamic-update-slice_fusion = bf16[16,5,4,128]{3,2,1,0:T(4,128)(2,1)} fusion(bf16[16,5,4,128]{3,2,1,0:T(4,128)(2,1)} %bitcast_dynamic-update-slice_fusion.1, bf16[16,1,4,128]{3,2,1,0:T(4,128)(2,1)S(1)} %stack.50), kind=kLoop, calls=%fused_computation.15 | loop fusion | bytes 32768
  3.1 0.6 %bitcast_dynamic-update-slice_fusion = bf16[16,5,4,128]{3,2,1,0:T(4,128)(2,1)} fusion(bf16[16,5,4,128]{3,2,1,0:T(4,128)(2,1)} %constant_dynamic-update-slice_fusion, bf16[16,4,128]{2,1,0:T(4,128)(2,1)S(1)} %reshape.22), kind=kLoop, calls=%fused_computation.11 | loop fusion | bytes 32768
  3.7 0.6 %bitcast_dynamic-update-slice_fusion.3 = bf16[16,5,4,128]{3,2,1,0:T(4,128)(2,1)} fusion(bf16[16,5,4,128]{3,2,1,0:T(4,128)(2,1)} %bitcast_dynamic-update-slice_fusion, bf16[16,4,128]{2,1,0:T(4,128)(2,1)S(1)} %reshape.22), kind=kLoop, calls=%fused_computation.14 | loop fusion | bytes 32768 | tf_op jit(solution)/shard_map/stack | solution.py:328
  4.3 7.3 %all-to-all-start = ((bf16[16,5,4,128]{3,2,1,0:T(4,128)(2,1)}), bf16[16,5,4,128]{3,2,1,0:T(4,128)(2,1)S(1)}, u32[]{:S(2)}, u32[]{:S(2)}) async-start(bf16[16,5,4,128]{3,2,1,0:T(4,128)(2,1)} %bitcast_dynamic-update-slice_fusion.3), calls=%async_computation | async-start | bytes 163840 | tf_op jit(solution)/shard_map/all_to_all | solution.py:329
  11.7 0.8 %fusion.2 = (bf16[3,3,8,128]{3,2,1,0:T(8,128)(2,1)S(1)}, bf16[3,3,8,128]{3,2,1,0:T(8,128)(2,1)S(1)}, bf16[3,3,8,128]{3,2,1,0:T(8,128)(2,1)S(1)}) fusion(bf16[3,3,3,3,96]{4,3,1,2,0:T(4,128)(2,1)} %bitcast.57), kind=kLoop, calls=%fused_computation.10 | loop fusion | bytes 70848 | tf_op jit(solution)/shard_map/squeeze | solution.py:346
  12.5 0.0 copy-done.2
  12.5 0.1 pad_maximum_fusion.2
  12.6 0.7 %copy.30 = bf16[3,3,4,8,256]{4,3,2,1,0:T(8,128)(2,1)} copy(bf16[3,3,4,8,256]{4,3,1,0,2:T(8,128)(2,1)S(1)} %pad_maximum_fusion) | data formatting | bytes 294912 | tf_op jit(solution)/shard_map/stack | solution.py:348
  13.3 0.6 %pad_maximum_fusion.1.gains_ref = f32[4,384]{1,0:T(4,128)} fusion(f32[1,384]{1,0:T(1,128)S(1)} %stack.57, f32[1,384]{1,0:T(1,128)S(1)} %stack.56, f32[1,384]{1,0:T(1,128)S(1)} %stack.55, f32[1,384]{1,0:T(1,128)S(1)} %stack.54), kind=kLoop, calls=%fused_computation.16 | loop fusion | flops 4608 | bytes 12288 | tf_op jit(solution)/shard_map/stack | solution.py:352
  13.9 4.0 %all-to-all-done = bf16[16,5,4,128]{3,2,1,0:T(4,128)(2,1)S(1)} async-done(((bf16[16,5,4,128]{3,2,1,0:T(4,128)(2,1)}), bf16[16,5,4,128]{3,2,1,0:T(4,128)(2,1)S(1)}, u32[]{:S(2)}, u32[]{:S(2)}) %all-to-all-start) | async-done | bytes 81952 | tf_op jit(solution)/shard_map/all_to_all | solution.py:329
  17.9 0.4 reshape.23
  18.3 0.8 %copy.27 = bf16[4,16,8,5,16]{4,3,2,1,0:T(8,128)(2,1)S(1)} copy(bf16[4,16,8,5,16]{4,2,1,0,3:T(8,128)(2,1)S(1)} %bitcast.52) | data formatting | bytes 163840 | tf_op jit(solution)/shard_map/transpose | solution.py:331
  19.2 0.5 reshape.24
  19.7 0.7 %pad.19.g_ref = bf16[4,128,128]{2,1,0:T(8,128)(2,1)} pad(bf16[4,128,80]{2,1,0:T(8,128)(2,1)S(1)} %reshape.24, bf16[]{:T(256)} %constant.4.clone.1), padding=0_0x0_0x0_48 | pad | bytes 212994 | tf_op jit(solution)/shard_map/jit(_pad)/pad | solution.py:333
  20.4 30.5 %shard_map.100 = f32[4,2,16,128]{3,2,1,0:T(8,128)} custom-call(bf16[4,128,128]{2,1,0:T(8,128)(2,1)} %pad.19.g_ref, f32[4,384]{1,0:T(4,128)} %pad_maximum_fusion.1.gains_ref, bf16[3,3,3,16,384]{4,3,2,1,0:T(8,128)(2,1)} %win_hbm.1, bf16[3,3456,384]{2,1,0:T(8,128)(2,1)} %bitcast.50, bf16[3,3,192,384]{3,2,1,0:T(8,128)(2,1)} %bitcast.53, ...), custom_call_target="tpu_custom_call" | custom-call | tf_op jit(solution)/shard_map/pallas_call | solution.py:356
  50.9 0.8 %slice.36 = f32[4,2,2,3,128]{4,3,2,1,0:T(4,128)S(1)} slice(f32[4,2,2,8,128]{4,3,2,1,0:T(8,128)} %bitcast.55), slice={[0:4], [0:2], [0:2], [0:3], [0:128]} | slice | bytes 49152 | tf_op jit(solution)/shard_map/slice | solution.py:392
  51.7 0.5 copy.35
  52.2 0.9 %copy.32 = f32[4,3,2,256]{3,2,1,0:T(2,128)} copy(f32[4,3,2,256]{0,3,2,1:T(8,128)S(1)} %bitcast.51) | data formatting | bytes 49152 | tf_op jit(solution)/shard_map/reshape | solution.py:393
  (14 shorter events, 0.1 us)
Async XLA Ops:
  0.0 12.5 %copy-start.2 = (f32[192]{0:T(256)S(1)}, f32[192]{0:T(256)}, u32[]{:S(2)}) copy-start(f32[192]{0:T(256)} %param.16) | copy-start | bytes 2308
  0.0 12.6 %copy-start.3 = (f32[96]{0:T(128)S(1)}, f32[96]{0:T(128)}, u32[]{:S(2)}) copy-start(f32[96]{0:T(128)} %param.18) | copy-start | bytes 1156
  0.0 12.6 %copy-start = (f32[384]{0:T(512)S(1)}, f32[384]{0:T(512)}, u32[]{:S(2)}) copy-start(f32[384]{0:T(512)} %param.14) | copy-start | bytes 4612
  0.0 12.6 %copy-start.1 = (f32[384]{0:T(512)S(1)}, f32[384]{0:T(512)}, u32[]{:S(2)}) copy-start(f32[384]{0:T(512)} %param.12) | copy-start | bytes 4612
  4.3 13.5 %all-to-all-start = ((bf16[16,5,4,128]{3,2,1,0:T(4,128)(2,1)}), bf16[16,5,4,128]{3,2,1,0:T(4,128)(2,1)S(1)}, u32[]{:S(2)}, u32[]{:S(2)}) async-start(bf16[16,5,4,128]{3,2,1,0:T(4,128)(2,1)} %bitcast_dynamic-update-slice_fusion.3), calls=%async_computation | async-start | bytes 163840 | tf_op jit(solution)/shard_map/all_to_all | solution.py:329
